TPU v7x, 256 devices: a whole 4x4x8 slice. The times are simulated.
256 devices in a mesh: row: 8 (over z), col: 4 (over y_lo, core), rep: 8 (over x, y_hi).
Axes of the slice: x: 4, y: 4 (y_hi: 2, y_lo: 2; y = y_hi * 2 + y_lo), z: 8, core: 2. Of those that a mesh axis runs over, the one named last changes fastest.
Arguments:
- upstream: float32 [16384, 16384], P('row', ('col', 'rep')), may hold values from -0.046875 to 0.046875
- input_panel: float32 [16384, 1024], P('row', ('col', 'rep')), may hold values from -6 to 6
Outputs:
- panel_grad: float32 [16384, 1024], P('row', ('col', 'rep'))
All inputs are finite; a program needn't handle non-finite values.
Results may differ from a plain program's by a relative error of at most 0.000071.
Values sent between devices are 32-bit elements; how exact they have to be, the bound alone decides.
A program may use at most 128 MiB of HBM per device.

v0:
```python
import jax
import jax.numpy as jnp
from jax import lax
from jax.sharding import PartitionSpec as P


def cut_along(x, dim, length):
    before, after = (x.shape[:dim], x.shape[dim + 1 :])
    return jnp.moveaxis(x.reshape(*before, length, -1, *after), dim, 0)


def summed_on_arrival(x, axis, dim):
    pieces = cut_along(x, dim, lax.axis_size(axis))
    arrived = lax.all_to_all(pieces, axis, split_axis=0, concat_axis=0, tiled=True)
    return arrived.sum(axis=0)


def joined_along(pieces, dim):
    dims = list(pieces.shape[1:])
    dims[dim] *= pieces.shape[0]
    return jnp.moveaxis(pieces, 0, dim).reshape(dims)


def copy_for_each(x, axis):
    copies = jnp.broadcast_to(x, (lax.axis_size(axis), *x.shape))
    return lax.all_to_all(copies, axis, split_axis=0, concat_axis=0, tiled=True)


def gathered_copies(x, axis, dim):
    return joined_along(copy_for_each(x, axis), dim)


def row_total(buffer):
    return summed_on_arrival(buffer, "row", 0)


def per_device(upstream, input_panel):
    precise = lax.Precision.HIGHEST
    row_count, col_count = upstream.shape
    width_slice = input_panel.shape[1]
    row_index = lax.axis_index("row")
    col_index = lax.axis_index(("col", "rep"))
    rows_global = row_index * row_count + lax.broadcasted_iota(jnp.int32, (row_count, col_count), 0)
    cols_global = col_index * col_count + lax.broadcasted_iota(jnp.int32, (row_count, col_count), 1)
    lower_tile = jnp.where(cols_global <= rows_global, upstream, jnp.float32(0.0))
    upper_part = lax.dot_general(
        lower_tile,
        lax.all_gather(input_panel, ("col", "rep"), axis=1, tiled=True),
        (((0,), (0,)), ((), ())),
        precision=precise,
        preferred_element_type=jnp.float32,
    )
    every_row = gathered_copies(input_panel, "row", 0)
    column_rows = lax.all_to_all(every_row, ("col", "rep"), split_axis=0, concat_axis=1, tiled=True)
    lower_part = jnp.dot(
        lower_tile, column_rows, precision=precise, preferred_element_type=jnp.float32
    )
    moved_lower, buffer = (
        lax.all_to_all(lower_part, ("col", "rep"), split_axis=1, concat_axis=0, tiled=True),
        lax.all_to_all(upper_part, ("col", "rep"), split_axis=1, concat_axis=0, tiled=True),
    )
    groups = moved_lower.shape[0] // row_count
    lower_sum = jnp.sum(moved_lower.reshape(groups, row_count, width_slice), axis=0)
    band_start = row_index * row_count
    current = lax.dynamic_slice_in_dim(buffer, band_start, row_count, 0)
    buffer = lax.dynamic_update_slice_in_dim(buffer, current + lower_sum, band_start, 0)
    return row_total(buffer)


def solution(mesh):
    placed = (P("row", ("col", "rep")), P("row", ("col", "rep")))
    return jax.shard_map(
        per_device, mesh=mesh, in_specs=placed, out_specs=P("row", ("col", "rep")), check_vma=False
    )
```

profile of v0, /device:TPU:1, one launch (start us, length us, event | category | flops | bytes accessed | tf_op | source)
XLA Modules:
  0.0 361.9 jit_solution(550470911194361348)
XLA Ops:
  6.5 0.0 all-gather.2.cloned.1.call-start
  6.5 0.7 all-gather.2.cloned.1.call-update
  7.3 1.2 broadcast_in_dim.8
  8.4 58.6 %all_to_all.58 = f32[8,2048,32]{1,2,0:T(8,128)S(1)} all-to-all(f32[8,2048,32]{1,2,0:T(8,128)S(1)} %broadcast_in_dim.8), channel_id=1, replica_groups=mesh['row'=8,'col'=4,'rep'=8] {'row'}, dimensions={0} | all-to-all | bytes 4194304 | tf_op jit(solution)/shard_map/all_to_all | solution.py:26
  67.1 1.2 copy.11
  68.3 1.7 all_to_all.47
  70.0 4.1 %copy.12 = f32[32,512,32]{1,2,0:T(8,128)} copy(f32[32,512,32]{1,0,2:T(8,128)} %all_to_all.47) | data formatting | bytes 4194304 | tf_op jit(solution)/shard_map/all_to_all | solution.py:54
  74.1 9.4 %all-to-all-start.2 = ((f32[32,512,32]{1,2,0:T(8,128)}), f32[32,512,32]{1,2,0:T(8,128)S(1)}, u32[]{:S(2)}, u32[]{:S(2)}) async-start(f32[32,512,32]{1,2,0:T(8,128)} %copy.12), calls=%async_computation.2 | async-start | bytes 4194304 | tf_op jit(solution)/shard_map/all_to_all | solution.py:54
  83.5 36.6 %all-to-all-done.2 = f32[32,512,32]{1,2,0:T(8,128)S(1)} async-done(((f32[32,512,32]{1,2,0:T(8,128)}), f32[32,512,32]{1,2,0:T(8,128)S(1)}, u32[]{:S(2)}, u32[]{:S(2)}) %all-to-all-start.2) | async-done | bytes 2097184 | tf_op jit(solution)/shard_map/all_to_all | solution.py:54
  120.1 17.8 %fusion = f32[2048,32,32]{0,2,1:T(8,128)} fusion(f32[2048,512]{1,0:T(8,128)} %param.2, f32[32,512,32]{1,2,0:T(8,128)S(1)} %all-to-all-done.2, s32[512]{0:T(512)S(1)} %iota_add_fusion.1, s32[2048]{0:T(1024)S(1)} %iota_add_fusion), kind=kOutput, calls=%fused_computation | convolution fusion | flops 12886999040 | bytes 14690304 | tf_op jit(solution)/shard_map/dot_general | solution.py:55
  137.9 4.9 %all-to-all-start.3 = ((f32[2048,32,32]{0,2,1:T(8,128)}), f32[2048,32,32]{0,2,1:T(8,128)}, u32[]{:S(2)}, u32[]{:S(2)}) async-start(f32[2048,32,32]{0,2,1:T(8,128)} %fusion), calls=%async_computation.3 | async-start | bytes 16777216 | tf_op jit(solution)/shard_map/all_to_all | solution.py:59
  142.9 0.0 all-gather.2.cloned.1.call-done
  142.9 18.7 %fusion.2 = f32[512,1024]{0,1:T(8,128)} fusion(f32[2048,1024]{0,1:T(8,128)} %all-gather.2.cloned.1.call-done, f32[2048,512]{1,0:T(8,128)} %param.2, s32[512]{0:T(512)S(1)} %iota_add_fusion.1, s32[2048]{0:T(1024)S(1)} %iota_add_fusion), kind=kOutput, calls=%fused_computation.3 | convolution fusion | flops 12886999040 | bytes 14690304 | tf_op jit(solution)/shard_map/dot_general | solution.py:46
  161.6 93.9 %all-to-all-done.3 = f32[2048,32,32]{0,2,1:T(8,128)} async-done(((f32[2048,32,32]{0,2,1:T(8,128)}), f32[2048,32,32]{0,2,1:T(8,128)}, u32[]{:S(2)}, u32[]{:S(2)}) %all-to-all-start.3) | async-done | bytes 8388640 | tf_op jit(solution)/shard_map/all_to_all | solution.py:59
  255.5 14.7 %all-to-all-start = ((f32[512,32,32]{0,2,1:T(8,128)}), f32[512,32,32]{0,2,1:T(8,128)S(1)}, u32[]{:S(2)}, u32[]{:S(2)}) async-start(f32[512,32,32]{0,2,1:T(8,128)} %bitcast.27), calls=%async_computation | async-start | bytes 4194304 | tf_op jit(solution)/shard_map/all_to_all | solution.py:60
  270.2 3.8 %reduce_sum.18 = f32[2048,32]{0,1:T(8,128)S(1)} reduce(f32[2048,32,32]{0,2,1:T(8,128)} %all-to-all-done.3, f32[]{:T(128)} %constant.21.clone.1), dimensions={1}, to_apply=%region_0.1 | reduce | flops 2031616 | bytes 8650756 | tf_op jit(solution)/shard_map/reduce_sum | solution.py:63
  274.1 25.5 %all-to-all-done = f32[512,32,32]{0,2,1:T(8,128)S(1)} async-done(((f32[512,32,32]{0,2,1:T(8,128)}), f32[512,32,32]{0,2,1:T(8,128)S(1)}, u32[]{:S(2)}, u32[]{:S(2)}) %all-to-all-start) | async-done | bytes 2097184 | tf_op jit(solution)/shard_map/all_to_all | solution.py:60
  299.6 0.2 copy.16
  299.9 0.2 copy.18
  300.1 54.1 %all_to_all.59 = f32[8,2048,32]{1,2,0:T(8,128)S(1)} all-to-all(f32[8,2048,32]{1,2,0:T(8,128)S(1)} %bitcast.26), channel_id=1, replica_groups=mesh['row'=8,'col'=4,'rep'=8] {'row'}, dimensions={0} | all-to-all | bytes 4194304 | tf_op jit(solution)/shard_map/all_to_all | solution.py:14
  354.2 0.8 reduce_sum.19
  (3 shorter events, 0.1 us)
Async XLA Ops:
  6.5 136.4 %all-gather.2.cloned.1.call-start = ((), (), s32[]{:S(2)}) async-start(), calls=%async_computation.5 | async-start | bytes 8650752 | tf_op jit(solution)/shard_map/all_gather | solution.py:48
  74.1 46.0 %all-to-all-start.2 = ((f32[32,512,32]{1,2,0:T(8,128)}), f32[32,512,32]{1,2,0:T(8,128)S(1)}, u32[]{:S(2)}, u32[]{:S(2)}) async-start(f32[32,512,32]{1,2,0:T(8,128)} %copy.12), calls=%async_computation.2 | async-start | bytes 4194304 | tf_op jit(solution)/shard_map/all_to_all | solution.py:54
  137.9 117.6 %all-to-all-start.3 = ((f32[2048,32,32]{0,2,1:T(8,128)}), f32[2048,32,32]{0,2,1:T(8,128)}, u32[]{:S(2)}, u32[]{:S(2)}) async-start(f32[2048,32,32]{0,2,1:T(8,128)} %fusion), calls=%async_computation.3 | async-start | bytes 16777216 | tf_op jit(solution)/shard_map/all_to_all | solution.py:59
  255.5 44.1 %all-to-all-start = ((f32[512,32,32]{0,2,1:T(8,128)}), f32[512,32,32]{0,2,1:T(8,128)S(1)}, u32[]{:S(2)}, u32[]{:S(2)}) async-start(f32[512,32,32]{0,2,1:T(8,128)} %bitcast.27), calls=%async_computation | async-start | bytes 4194304 | tf_op jit(solution)/shard_map/all_to_all | solution.py:60
Sparse Core Ops, SparseCore 0:
  9.1 117.0 all-gather.1
where the time goes:
time: 362 us
  waiting for transfers between devices  157 us (43%)
  blocking collectives  113 us (31%)
  matrix products  36.5 us (10%)
  starting transfers between devices  29.1 us (8%)
  between operations  13.5 us (4%)
  local copies, waits for them, and re-layouts  8.61 us (2%)
  other arithmetic  4.7 us (1%)
    all_to_all x1, waiting for transfers between devices, per_device(): lax.all_to_all(lower_part, ('col', 'rep'), split_axis=1, concat_axis=0, t...  93.9 us
    all_to_all x1, blocking collectives, copy_for_each(): return lax.all_to_all(copies, axis, split_axis=0, concat_axis=0, tiled=True)  58.6 us
    all_to_all x1, blocking collectives, summed_on_arrival(): lax.all_to_all(pieces, axis, split_axis=0, concat_axis=0, tiled=True)  54.1 us
    all_to_all x1, waiting for transfers between devices, per_device(): lax.all_to_all(every_row, ('col', 'rep'), split_axis=0, concat_axis=1, ti...  36.6 us
    all_to_all x1, waiting for transfers between devices, per_device(): lax.all_to_all(upper_part, ('col', 'rep'), split_axis=1, concat_axis=0, t...  25.5 us
    dot_general x1, matrix products, per_device(): lax.dot_general(lower_tile, lax.all_gather(input_panel, ('col', 'rep'), a...  18.7 us
    dot_general x1, matrix products, per_device(): jnp.dot(lower_tile, column_rows, precision=precise, preferred_element_typ...  17.8 us
    all_to_all x1, starting transfers between devices, per_device(): lax.all_to_all(upper_part, ('col', 'rep'), split_axis=1, concat_axis=0, t...  14.7 us
  transfers between devices with their start and end apart: 4, of which 3 were waited for; matrix products, arithmetic and copies ran while one was open for 13% of the time, Pallas kernels for 0%

commit v1 on v0

v1 whole, which is shorter than its diff:
```python
import functools

import jax
import jax.numpy as jnp
from jax import lax
from jax.experimental import pallas as pl
from jax.experimental.pallas import tpu as pltpu
from jax.sharding import PartitionSpec as P

MESH = pl.DeviceIdType.MESH
ROWS = 2048
COLS = 512
HALF = ROWS // 2
CHUNKS = 4
WIDE = 256
PIECES = 16
PART = 64
DEPTH = 5
SKEW = 2
AWAY = (0, 3, 1, 2)
EXCHANGE = 22


def at(start, length, step):
    return pl.ds(pl.multiple_of(start, step), length)


def halves(x):
    high = x.astype(jnp.bfloat16)
    return high, (x - high.astype(jnp.float32)).astype(jnp.bfloat16)


def kernel(
    upstream, panel, out,
    gathered, block, upper_sum, upper_in, lower_sum,
    in_partner, in_far, in_near, in_cross_far, in_cross,
    tile, tile_high, tile_low, left_high, left_low, right_high, right_low,
    send_sem, recv_sem, z_send, z_down, z_up, local_sem,
):
    row, col, rep = lax.axis_index("row"), lax.axis_index("col"), lax.axis_index("rep")
    core, x = lax.rem(col, 2), lax.div(rep, 2)
    y = lax.rem(rep, 2) * 2 + lax.div(col, 2)
    me = col * 8 + rep

    def chip(order, first, second):
        dx, dy = (first, second) if order == 0 else (second, first)
        return lax.rem(x + dx, 4), lax.rem(y + dy, 4)

    def number(place, on):
        return (lax.rem(place[1], 2) * 2 + on) * 8 + place[0] * 2 + lax.div(place[1], 2)

    def device(place, on):
        return (row, lax.rem(place[1], 2) * 2 + on, place[0] * 2 + lax.div(place[1], 2))

    low = lax.div(col, 2) * 4 + lax.div(x, 2)
    high = low + 2
    source = jnp.where(core == 0, low, high)
    offset = lax.rem(me, 4) * COLS
    active = row >= source
    root = row == source
    below = row > source
    upward = (core == 1) | (row <= high)
    child_up = ((core == 0) & (row >= low) & (row < high)) | ((core == 1) & (row >= high) & (row < 7))
    child_down = (core == 0) & ((root & (high < 7)) | (row > high + 1))
    depth = jnp.where(upward, row - source, 8 - row)
    above = jnp.where(upward, row - 1, jnp.where(row == 7, low, row + 1))
    up_device = (row + 1, col, rep)
    down_device = (jnp.where(root, 7, row - 1), col, rep)
    above_device = (above, col, rep)
    slot = jnp.where(upward, 0, 1)

    def copy(src, dst, which, to):
        return pltpu.make_async_remote_copy(
            src_ref=src, dst_ref=dst, send_sem=send_sem.at[which], recv_sem=recv_sem.at[which],
            device_id=to, device_id_type=MESH,
        )

    sent = []

    def send(src, dst, which, to):
        one = copy(src, dst, which, to)
        one.start()
        sent.append(one)

    partner = device((x, y), 1 - core)

    def arrived(dst, which):
        copy(dst, dst, which, partner).wait_recv()

    first_cols, second_cols, all_cols = pl.ds(0, HALF), pl.ds(HALF, HALF), pl.ds(0, ROWS)

    def slab(q, place, cols=all_cols):
        return gathered.at[at(q * WIDE + number(place, core) * 8, 8, 8), cols]

    def total(q, place, cols=all_cols):
        return lower_sum.at[at(q * WIDE + number(place, core) * 8, 8, 8), cols]

    def group(ref, q, half, on):
        return ref.at[at(q * WIDE + half * 128 + on * 64, 64, 8), :]

    def gather_own_first(q):
        order, base = q % 2, q * EXCHANGE
        own = panel.at[pl.ds(q * 8, 8), :]
        send(own, slab(q, (x, y)), base + 0, device(chip(order, 1, 0), core))
        send(own, slab(q, (x, y)), base + 1, device(chip(order, 3, 0), core))

    def gather_own_second(q):
        order, base = q % 2, q * EXCHANGE
        own = panel.at[pl.ds(q * 8, 8), :]
        send(own, slab(q, (x, y)), base + 4, device(chip(order, 0, 1), core))
        send(own, slab(q, (x, y)), base + 5, device(chip(order, 0, 3), core))

    def gather_across(q, j):
        order, base = q % 2, q * EXCHANGE + 4 + 2 * j
        piece = slab(q, chip(order, AWAY[j], 0))
        send(piece, piece, base + 0, device(chip(order, 0, 1), core))
        send(piece, piece, base + 1, device(chip(order, 0, 3), core))

    def gather_first(q):
        order, base = q % 2, q * EXCHANGE
        arrived(slab(q, chip(order, 3, 0)), base + 0)
        piece = slab(q, chip(order, 3, 0), first_cols)
        send(piece, piece, base + 2, device(chip(order, 1, 0), core))
        gather_across(q, 1)
        arrived(slab(q, chip(order, 1, 0)), base + 1)
        piece = slab(q, chip(order, 1, 0), second_cols)
        send(piece, piece, base + 3, device(chip(order, 3, 0), core))
        gather_across(q, 2)

    def gather_opposite(q):
        order, base = q % 2, q * EXCHANGE
        arrived(slab(q, chip(order, 2, 0), first_cols), base + 2)
        arrived(slab(q, chip(order, 2, 0), second_cols), base + 3)
        gather_across(q, 3)

    def gather_forward(q, j):
        order, base = q % 2, q * EXCHANGE + 4 + 2 * j
        arrived(slab(q, chip(order, AWAY[j], 3)), base + 0)
        piece = slab(q, chip(order, AWAY[j], 3), first_cols)
        send(piece, piece, base + 8, device(chip(order, 0, 1), core))
        arrived(slab(q, chip(order, AWAY[j], 1)), base + 1)
        piece = slab(q, chip(order, AWAY[j], 1), second_cols)
        send(piece, piece, base + 9, device(chip(order, 0, 3), core))

    def gather_last(q):
        order, base = q % 2, q * EXCHANGE + 12
        for j in range(4):
            arrived(slab(q, chip(order, AWAY[j], 2), first_cols), base + 2 * j)
            arrived(slab(q, chip(order, AWAY[j], 2), second_cols), base + 2 * j + 1)
        for half in range(2):
            piece = group(gathered, q, half, core)
            send(piece, piece, q * EXCHANGE + 20 + half, partner)

    def gather_done(q):
        for half in range(2):
            arrived(group(gathered, q, half, 1 - core), q * EXCHANGE + 20 + half)

    def part(ref, k, more=0):
        return ref.at[at(more + k * PART, PART, PART), :]

    def z_copy(src, k, way, to):
        return pltpu.make_async_remote_copy(
            src_ref=src, dst_ref=part(block, k), send_sem=z_send.at[way * PIECES + k], recv_sem=z_down.at[k],
            device_id=to, device_id_type=MESH,
        )

    def z_start(q):
        @pl.when(root)
        def _():
            def one(i, carry):
                k = q * 4 + i
                src = gathered.at[at(k * PART, PART, PART), at(offset, COLS, COLS)]

                @pl.when(child_up)
                def _():
                    z_copy(src, k, 0, up_device).start()

                @pl.when(child_down)
                def _():
                    z_copy(src, k, 1, down_device).start()

                return carry

            lax.fori_loop(0, 4, one, 0)

    def z_round(step):
        k = step - SKEW * (depth - 1)

        @pl.when(below & (k >= 0) & (k < PIECES))
        def _():
            src = part(block, k)
            z_copy(src, k, 0, up_device).wait_recv()

            @pl.when(child_up)
            def _():
                z_copy(src, k, 0, up_device).start()

            @pl.when(child_down)
            def _():
                z_copy(src, k, 1, down_device).start()

    def sum_copy(k, which):
        return pltpu.make_async_remote_copy(
            src_ref=part(upper_sum, k), dst_ref=part(upper_in, k, which * PIECES * PART),
            send_sem=z_send.at[2 * PIECES + k], recv_sem=z_up.at[which * PIECES + k],
            device_id=above_device, device_id_type=MESH,
        )

    def sum_round(step):
        k = step - SKEW * (DEPTH - depth)

        @pl.when(active & (k >= 0) & (k < PIECES))
        def _():
            for which, there in enumerate((child_up, child_down)):
                @pl.when(there)
                def _():
                    sum_copy(k, which).wait_recv()
                    mine = at(k * PART, PART, PART)
                    other = at(which * PIECES * PART + k * PART, PART, PART)
                    upper_sum[mine, :] = upper_sum[mine, :] + upper_in[other, :]

            @pl.when(below)
            def _():
                sum_copy(k, slot).start()

    def prepare():
        def one(n, carry):
            rows = at(n * 256, 256, 256)
            pltpu.make_async_copy(upstream.at[rows, :], tile.at[rows, :], local_sem.at[n]).wait()
            row_number = row * ROWS + n * 256 + lax.broadcasted_iota(jnp.int32, (256, COLS), 0)
            col_number = me * COLS + lax.broadcasted_iota(jnp.int32, (256, COLS), 1)
            kept = jnp.where(col_number <= row_number, tile[rows, :], 0.0)
            tile_high[rows, :], tile_low[rows, :] = halves(kept)
            return carry

        lax.fori_loop(0, 8, one, 0)

        @pl.when(jnp.logical_not(active))
        def _():
            def clear(n, carry):
                lower_sum[at(n * 64, 64, 64), :] = jnp.zeros((64, ROWS), jnp.float32)
                return carry

            lax.fori_loop(0, 16, clear, 0)

    def product(left_a, left_b, right_a, right_b, dims):
        dot = functools.partial(
            lax.dot_general, dimension_numbers=(dims, ((), ())), preferred_element_type=jnp.float32
        )
        return dot(left_a, right_a) + dot(left_b, right_a) + dot(left_a, right_b)

    def upper(q):
        @pl.when(active)
        def _():
            here = pl.ds(q * WIDE, WIDE)

            def cut(n, carry):
                cols = at(n * 256, 256, 256)
                left_high[:, cols], left_low[:, cols] = halves(gathered[here, cols])
                return carry

            lax.fori_loop(0, 8, cut, 0)

            def one(n, carry):
                cols = at(n * 256, 256, 256)
                upper_sum[here, cols] = product(
                    left_high[...], left_low[...], tile_high[:, cols], tile_low[:, cols], ((1,), (0,))
                )
                return carry

            lax.fori_loop(0, 2, one, 0)

    def lower(q):
        @pl.when(active)
        def _():
            here = pl.ds(q * WIDE, WIDE)

            @pl.when(root)
            def _():
                right_high[...], right_low[...] = halves(gathered[here, at(offset, COLS, COLS)])

            @pl.when(below)
            def _():
                right_high[...], right_low[...] = halves(block[here, :])

            def one(n, carry):
                rows = at(n * 256, 256, 256)
                lower_sum[here, rows] = product(
                    right_high[...], right_low[...], tile_high[rows, :], tile_low[rows, :], ((1,), (1,))
                )
                return carry

            lax.fori_loop(0, 8, one, 0)

    def scatter_partner(q):
        @pl.when(root)
        def _():
            here, cols = pl.ds(q * WIDE, WIDE), at(offset, COLS, COLS)
            lower_sum[here, cols] = lower_sum[here, cols] + upper_sum[here, :]

        for half in range(2):
            send(
                group(lower_sum, q, half, 1 - core), in_partner.at[pl.ds((q * 2 + half) * 64, 64), :],
                (CHUNKS + q) * EXCHANGE + half, partner,
            )

    def scatter_far(q):
        order, base = q % 2, (CHUNKS + q) * EXCHANGE
        for half in range(2):
            came = pl.ds((q * 2 + half) * 64, 64)
            arrived(in_partner.at[came, :], base + half)
            mine = at(q * WIDE + half * 128 + core * 64, 64, 8)
            lower_sum[mine, :] = lower_sum[mine, :] + in_partner[came, :]
        for j in (3, 1, 2, 0):
            to = chip(order, AWAY[j], 2)
            for way, cols in enumerate((first_cols, second_cols)):
                send(
                    total(q, to, cols), in_far.at[pl.ds((q * 8 + 2 * j + way) * 8, 8), :],
                    base + 2 + 2 * j + way, device(chip(order, 0, 1 if way == 0 else 3), core),
                )

    def scatter_near(q):
        order, base = q % 2, (CHUNKS + q) * EXCHANGE
        for j in (3, 1, 2, 0):
            for way, cols in enumerate((first_cols, second_cols)):
                step = 1 if way == 0 else 3
                to = chip(order, AWAY[j], step)
                came = pl.ds((q * 8 + 2 * j + way) * 8, 8)
                arrived(in_far.at[came, :], base + 2 + 2 * j + way)
                mine = at(q * WIDE + number(to, core) * 8, 8, 8)
                lower_sum[mine, cols] = lower_sum[mine, cols] + in_far[came, :]
                send(
                    total(q, to), in_near.at[came, :], base + 10 + 2 * j + way,
                    device(chip(order, 0, step), core),
                )

    def scatter_column(q):
        order, base = q % 2, (CHUNKS + q) * EXCHANGE
        for j in (3, 1, 2, 0):
            mine = at(q * WIDE + number(chip(order, AWAY[j], 0), core) * 8, 8, 8)
            first, second = (pl.ds((q * 8 + 2 * j + way) * 8, 8) for way in range(2))
            arrived(in_near.at[first, :], base + 10 + 2 * j)
            arrived(in_near.at[second, :], base + 10 + 2 * j + 1)
            lower_sum[mine, :] = lower_sum[mine, :] + (in_near[first, :] + in_near[second, :])
            if j == 3:
                for way, cols in enumerate((first_cols, second_cols)):
                    send(
                        total(q, chip(order, 2, 0), cols), in_cross_far.at[pl.ds((q * 2 + way) * 8, 8), :],
                        base + 18 + way, device(chip(order, 1 if way == 0 else 3, 0), core),
                    )

    def scatter_row(q):
        order, base = q % 2, (CHUNKS + q) * EXCHANGE
        for way, cols in enumerate((first_cols, second_cols)):
            step = 1 if way == 0 else 3
            to = chip(order, step, 0)
            came = pl.ds((q * 2 + way) * 8, 8)
            arrived(in_cross_far.at[came, :], base + 18 + way)
            mine = at(q * WIDE + number(to, core) * 8, 8, 8)
            lower_sum[mine, cols] = lower_sum[mine, cols] + in_cross_far[came, :]
            send(total(q, to), in_cross.at[came, :], base + 20 + way, device(to, core))

    def scatter_done(q):
        base = (CHUNKS + q) * EXCHANGE
        first, second = (pl.ds((q * 2 + way) * 8, 8) for way in range(2))
        arrived(in_cross.at[first, :], base + 20)
        arrived(in_cross.at[second, :], base + 21)
        mine = at(q * WIDE + me * 8, 8, 8)
        out[pl.ds(q * 8, 8), :] = lower_sum[mine, :] + (in_cross[first, :] + in_cross[second, :])

    def fetch(n, carry):
        rows = at(n * 256, 256, 256)
        pltpu.make_async_copy(upstream.at[rows, :], tile.at[rows, :], local_sem.at[n]).start()
        return carry

    lax.fori_loop(0, 8, fetch, 0)
    for q in range(CHUNKS):
        gathered[at(q * WIDE + me * 8, 8, 8), :] = panel[pl.ds(q * 8, 8), :]

    barrier = pltpu.get_barrier_semaphore()
    for first, second in ((1, 0), (3, 0), (0, 1), (0, 3)):
        pl.semaphore_signal(barrier, inc=1, device_id=device(chip(0, first, second), core), device_id_type=MESH)
    pl.semaphore_signal(barrier, inc=1, device_id=partner, device_id_type=MESH)
    for there, to in ((below, above_device), (child_up, up_device), (child_down, down_device)):
        @pl.when(there)
        def _():
            pl.semaphore_signal(barrier, inc=1, device_id=to, device_id_type=MESH)

    pl.semaphore_wait(barrier, 5 + sum(jnp.where(there, 1, 0) for there in (below, child_up, child_down)))

    def steps(pair):
        a, b = pair
        return [
            lambda: (gather_first(a), gather_first(b)),
            lambda: (gather_forward(a, 0), gather_forward(b, 0)),
            lambda: (gather_opposite(a), gather_opposite(b)),
            lambda: (gather_forward(a, 1), gather_forward(b, 1)),
            lambda: (gather_forward(a, 2), gather_forward(b, 2)),
            lambda: (gather_forward(a, 3), gather_forward(b, 3)),
            lambda: (gather_last(a), gather_last(b)),
            lambda: (gather_done(a), gather_done(b)),
        ]

    def begin(pair):
        for q in pair:
            gather_own_first(q)
        for q in pair:
            gather_own_second(q)

    begin((0, 1))
    prepare()
    early = steps((0, 1))
    for n, step in enumerate(early):
        if n == 5:
            begin((2, 3))
        step()
    z_start(0)
    z_start(1)

    plan = {}

    def add(n, task):
        plan.setdefault(n, []).append(task)

    add(0, lambda: upper(0))
    for n, step in enumerate(steps((2, 3))):
        add(n, step)
    add(2, lambda: upper(1))
    add(7, lambda: (z_start(2), z_start(3)))
    add(8, lambda: upper(2))
    add(9, lambda: upper(3))
    stages = (scatter_partner, scatter_far, scatter_near, scatter_column, scatter_row, scatter_done)
    for q in range(CHUNKS):
        add(12 + 4 * q, functools.partial(lower, q))
        for n, stage in enumerate(stages):
            add(14 + 4 * q + n, functools.partial(stage, q))
    rounds = PIECES + SKEW * DEPTH
    for n in range(max(plan) + 1):
        if n < rounds:
            z_round(n)
        for task in plan.get(n, ()):
            task()
        if n < rounds:
            sum_round(n)

    for one in sent:
        one.wait_send()

    def settle(k, carry):
        @pl.when(child_up)
        def _():
            z_copy(part(block, k), k, 0, up_device).wait_send()

        @pl.when(child_down)
        def _():
            z_copy(part(block, k), k, 1, down_device).wait_send()

        @pl.when(below)
        def _():
            sum_copy(k, 0).wait_send()

        return carry

    lax.fori_loop(0, PIECES, settle, 0)


def per_device(upstream, input_panel):
    f32, bf16 = jnp.float32, jnp.bfloat16
    total = CHUNKS * WIDE
    vmem = pltpu.VMEM
    result = pl.pallas_call(
        kernel,
        out_shape=jax.ShapeDtypeStruct((32, ROWS), f32),
        in_specs=[pl.BlockSpec(memory_space=pl.ANY), pl.BlockSpec(memory_space=pltpu.VMEM)],
        out_specs=pl.BlockSpec(memory_space=pltpu.VMEM),
        scratch_shapes=[
            vmem((total, ROWS), f32),
            vmem((total, COLS), f32),
            vmem((total, COLS), f32),
            vmem((2 * total, COLS), f32),
            vmem((total, ROWS), f32),
            vmem((total // 2, ROWS), f32),
            vmem((CHUNKS * 64, HALF), f32),
            vmem((CHUNKS * 64, ROWS), f32),
            vmem((CHUNKS * 16, HALF), f32),
            vmem((CHUNKS * 16, ROWS), f32),
            vmem((ROWS, COLS), f32),
            vmem((ROWS, COLS), bf16),
            vmem((ROWS, COLS), bf16),
            vmem((WIDE, ROWS), bf16),
            vmem((WIDE, ROWS), bf16),
            vmem((WIDE, COLS), bf16),
            vmem((WIDE, COLS), bf16),
            pltpu.SemaphoreType.DMA((2 * CHUNKS * EXCHANGE,)),
            pltpu.SemaphoreType.DMA((2 * CHUNKS * EXCHANGE,)),
            pltpu.SemaphoreType.DMA((3 * PIECES,)),
            pltpu.SemaphoreType.DMA((PIECES,)),
            pltpu.SemaphoreType.DMA((2 * PIECES,)),
            pltpu.SemaphoreType.DMA((8,)),
        ],
        compiler_params=pltpu.CompilerParams(
            collective_id=0, has_side_effects=True, vmem_limit_bytes=60 * 1024 * 1024
        ),
    )(upstream, input_panel.T)
    return result.T


def solution(mesh):
    placed = (P("row", ("col", "rep")), P("row", ("col", "rep")))
    return jax.shard_map(
        per_device, mesh=mesh, in_specs=placed, out_specs=P("row", ("col", "rep")), check_vma=False
    )
```

time: 362 us -> 144 us (0.40)
  waiting for transfers between devices: 157 us -> 0 us
  Pallas kernels: 0 us -> 142 us
  blocking collectives: 113 us -> 0 us
  matrix products: 36.5 us -> 0 us
  starting transfers between devices: 29.1 us -> 0 us
  between operations: 13.5 us -> 0.01 us
  local copies, waits for them, and re-layouts: 8.61 us -> 1.67 us
  other arithmetic: 4.7 us -> 0 us
    all_to_all x3 -> x0, waiting for transfers between devices: 156 us -> none  [the longest x1 93.9 us: per_device(): lax.all_to_all(lower_part, ('col', 'rep'), split_axis=1, concat_axis=0, t...]
    pallas_call x0 -> x1, Pallas kernels: none -> 142 us  [per_device(): pl.pallas_call(kernel, out_shape=jax.ShapeDtypeStruct((32, ROWS), f32), i...]
    all_to_all x2 -> x0, blocking collectives: 113 us -> none  [the longest x1 58.6 us: copy_for_each(): return lax.all_to_all(copies, axis, split_axis=0, concat_axis=0, tiled=True)]
    dot_general x2 -> x0, matrix products: 36.5 us -> none  [the longest x1 18.7 us: per_device(): lax.dot_general(lower_tile, lax.all_gather(input_panel, ('col', 'rep'), a...]
    all_to_all x3 -> x0, starting transfers between devices: 29.1 us -> none  [the longest x1 14.7 us: per_device(): lax.all_to_all(upper_part, ('col', 'rep'), split_axis=1, concat_axis=0, t...]
    all_to_all x4 -> x0, local copies, waits for them, and re-layouts: 7.22 us -> none  [the longest x2 5.81 us: per_device(): lax.all_to_all(every_row, ('col', 'rep'), split_axis=0, concat_axis=1, ti...]
    reduce_sum x2 -> x0, other arithmetic: 4.64 us -> none  [the longest x1 3.82 us: per_device(): jnp.sum(moved_lower.reshape(groups, row_count, width_slice), axis=0)]
  transfers between devices with their start and end apart: 4 -> 0, of which waited for: 3 -> 0; matrix products, arithmetic and copies ran while one was open for 13% -> 0% of each run, Pallas kernels for 0% -> 0%
where the time goes in v1:
time: 144 us; the launch traced here: 143 us
  Pallas kernels  142 us (99%)
  local copies, waits for them, and re-layouts  1.67 us (1%)
    pallas_call x1, Pallas kernels, per_device(): pl.pallas_call(kernel, out_shape=jax.ShapeDtypeStruct((32, ROWS), f32), i...  142 us

profile of v1, /device:TPU:1, one launch (start us, length us, event | category | flops | bytes accessed | tf_op | source)
XLA Modules:
  0.0 143.3 jit_solution(3365961280897190788)
XLA Ops:
  0.0 141.6 %shard_map.28 = f32[32,2048]{1,0:T(8,128)} custom-call(f32[2048,512]{1,0:T(8,128)} %upstream.1, f32[32,2048]{1,0:T(8,128)} %bitcast.3), custom_call_target="tpu_custom_call" | custom-call | tf_op jit(solution)/shard_map/pallas_call | solution.py:471
  141.6 1.7 %copy.4 = f32[2048,32]{0,1:T(8,128)} copy(f32[2048,32]{0,1:T(8,128)} %bitcast.2) | data formatting | bytes 524288

commit v2 on v1

v2 whole, which is shorter than its diff:
```python
import functools

import jax
import jax.numpy as jnp
from jax import lax
from jax.experimental import pallas as pl
from jax.experimental.pallas import tpu as pltpu
from jax.sharding import PartitionSpec as P

MESH = pl.DeviceIdType.MESH
ROWS = 2048
COLS = 512
HALF = ROWS // 2
CHUNKS = 4
WIDE = 256
PIECES = 32
PART = 32
PACK = 2
DEPTH = 5
SKEW = 3
AWAY = (0, 3, 1, 2)
STAGES = 20
LANES = 2 * CHUNKS * STAGES
COPIES = 2 * LANES + 6 * CHUNKS


def at(start, length, step):
    return pl.ds(pl.multiple_of(start, step), length)


def halves(x):
    high = x.astype(jnp.bfloat16)
    return high, (x - high.astype(jnp.float32)).astype(jnp.bfloat16)


def kernel(
    upstream, panel, out,
    gathered, block, upper_sum, upper_in, lower_sum,
    in_partner, in_far, in_near, in_cross_far, in_cross, in_root,
    tile, tile_high, tile_low, left_high, left_low, right_high, right_low,
    send_sem, recv_sem, z_send, z_down, z_up, root_send, root_recv, local_sem,
):
    row, col, rep = lax.axis_index("row"), lax.axis_index("col"), lax.axis_index("rep")
    core, x = lax.rem(col, 2), lax.div(rep, 2)
    y = lax.rem(rep, 2) * 2 + lax.div(col, 2)
    me = col * 8 + rep

    xs = [x] + [lax.rem(x + d, 4) for d in (1, 2, 3)]
    ys = [y] + [lax.rem(y + d, 4) for d in (1, 2, 3)]
    cols = [lax.rem(v, 2) * 2 for v in ys]
    reps = [[u * 2 + lax.div(v, 2) for v in ys] for u in xs]
    mine_at = [[((cols[b] + core) * 8 + reps[a][b]) * 8 for b in range(4)] for a in range(4)]

    def chip(order, first, second):
        return (first, second) if order == 0 else (second, first)

    def number(place):
        return mine_at[place[0]][place[1]]

    def device(place, on):
        return (row, cols[place[1]] + on, reps[place[0]][place[1]])

    low = lax.div(col, 2) * 4 + lax.div(x, 2)
    high = low + 2
    source = jnp.where(core == 0, low, high)
    offset = lax.rem(me, 4) * COLS
    active = row >= source
    root = row == source
    relay = (core == 0) & (low == 4) & (row == 2)
    below = (row > source) | relay
    member = active | relay
    upward = (core == 1) | (row <= high)
    child_up = ((core == 0) & (row >= low) & (row < high)) | ((core == 1) & (row >= high) & (row < 7))
    child_down = ((core == 0) & ((root & (high < 7)) | (row > high + 1))) | relay
    depth = jnp.where(relay, 1, jnp.where(upward, row - source, 8 - row + jnp.where(low == 4, 1, 0)))
    above = jnp.where(relay, 4, jnp.where(upward, row - 1, jnp.where(row < 7, row + 1, jnp.where(low == 4, 2, low))))
    up_device = (row + 1, col, rep)
    down_device = (jnp.where(root & (low == 4), 2, jnp.where(root | relay, 7, row - 1)), col, rep)
    above_device = (above, col, rep)
    slot = jnp.where(upward & jnp.logical_not(relay), 0, 1)

    def copy(src, dst, which, to):
        return pltpu.make_async_remote_copy(
            src_ref=src, dst_ref=dst, send_sem=send_sem.at[which], recv_sem=recv_sem.at[which],
            device_id=to, device_id_type=MESH,
        )

    sent = []

    def send(src, dst, which, to):
        one = copy(src, dst, which, to)
        one.start()
        sent.append(one)

    partner = (row, col + 1 - 2 * core, rep)

    def arrived(dst, which):
        copy(dst, dst, which, partner).wait_recv()

    def columns(h):
        return pl.ds(h * HALF, HALF)

    def quarter(h, way):
        return pl.ds(h * HALF + way * (HALF // 2), HALF // 2)

    def slab(q, place, cols):
        return gathered.at[at(q * WIDE + number(place), 8, 8), cols]

    def total(q, place, cols):
        return lower_sum.at[at(q * WIDE + number(place), 8, 8), cols]

    def group(ref, q, half, on):
        return ref.at[at(q * WIDE + half * 128 + on * 64, 64, 8), :]

    def gather_own(q):
        own = panel.at[pl.ds(q * 8, 8), :]
        for axis in range(2):
            for h in range(2):
                base, cols = (2 * q + h) * STAGES, columns(h)
                for way, step in enumerate((1, 3)):
                    to = chip(h, step, 0) if axis == 0 else chip(h, 0, step)
                    send(own.at[:, cols], slab(q, (0, 0), cols), base + (0 if axis == 0 else 4) + way, device(to, core))

    def gather_across(q, h, j):
        base = (2 * q + h) * STAGES + 4 + 2 * j
        piece = slab(q, chip(h, AWAY[j], 0), columns(h))
        send(piece, piece, base + 0, device(chip(h, 0, 1), core))
        send(piece, piece, base + 1, device(chip(h, 0, 3), core))

    def gather_first(q):
        for h in range(2):
            base = (2 * q + h) * STAGES
            arrived(slab(q, chip(h, 3, 0), columns(h)), base + 0)
            piece = slab(q, chip(h, 3, 0), quarter(h, 0))
            send(piece, piece, base + 2, device(chip(h, 1, 0), core))
            arrived(slab(q, chip(h, 1, 0), columns(h)), base + 1)
            piece = slab(q, chip(h, 1, 0), quarter(h, 1))
            send(piece, piece, base + 3, device(chip(h, 3, 0), core))
        for h in range(2):
            gather_across(q, h, 1)
            gather_across(q, h, 2)

    def gather_opposite(q):
        for h in range(2):
            base = (2 * q + h) * STAGES
            arrived(slab(q, chip(h, 2, 0), quarter(h, 0)), base + 2)
            arrived(slab(q, chip(h, 2, 0), quarter(h, 1)), base + 3)
            gather_across(q, h, 3)

    def gather_forward(q, j):
        for h in range(2):
            base = (2 * q + h) * STAGES + 4 + 2 * j
            arrived(slab(q, chip(h, AWAY[j], 3), columns(h)), base + 0)
            piece = slab(q, chip(h, AWAY[j], 3), quarter(h, 0))
            send(piece, piece, base + 8, device(chip(h, 0, 1), core))
            arrived(slab(q, chip(h, AWAY[j], 1), columns(h)), base + 1)
            piece = slab(q, chip(h, AWAY[j], 1), quarter(h, 1))
            send(piece, piece, base + 9, device(chip(h, 0, 3), core))

    def gather_last(q):
        for h in range(2):
            base = (2 * q + h) * STAGES + 12
            for j in range(4):
                arrived(slab(q, chip(h, AWAY[j], 2), quarter(h, 0)), base + 2 * j)
                arrived(slab(q, chip(h, AWAY[j], 2), quarter(h, 1)), base + 2 * j + 1)
        for half in range(2):
            piece = group(gathered, q, half, core)
            send(piece, piece, 2 * LANES + 2 * q + half, partner)

    def gather_done(q):
        for half in range(2):
            arrived(group(gathered, q, half, 1 - core), 2 * LANES + 2 * q + half)

    def part(ref, k, more=0):
        return ref.at[at(more + k * PART, PART, PART), :]

    def z_copy(src, k, way, to):
        return pltpu.make_async_remote_copy(
            src_ref=src, dst_ref=part(block, k), send_sem=z_send.at[way * PIECES + k], recv_sem=z_down.at[k],
            device_id=to, device_id_type=MESH,
        )

    def z_start(q):
        @pl.when(root)
        def _():
            def one(i, carry):
                k = q * (PIECES // CHUNKS) + i
                src = gathered.at[at(k * PART, PART, PART), at(offset, COLS, COLS)]

                @pl.when(child_up)
                def _():
                    z_copy(src, k, 0, up_device).start()

                @pl.when(child_down)
                def _():
                    z_copy(src, k, 1, down_device).start()

                return carry

            lax.fori_loop(0, PIECES // CHUNKS, one, 0)

    def z_round(step):
        first = (step - SKEW * (depth - 1)) * PACK

        @pl.when(below & (first >= 0) & (first < PIECES))
        def _():
            def one(i, carry):
                k = first + i
                src = part(block, k)
                z_copy(src, k, 0, up_device).wait_recv()

                @pl.when(child_up)
                def _():
                    z_copy(src, k, 0, up_device).start()

                @pl.when(child_down)
                def _():
                    z_copy(src, k, 1, down_device).start()

                return carry

            lax.fori_loop(0, PACK, one, 0)

    def sum_copy(k, which):
        return pltpu.make_async_remote_copy(
            src_ref=part(upper_sum, k), dst_ref=part(upper_in, k, which * PIECES * PART),
            send_sem=z_send.at[2 * PIECES + k], recv_sem=z_up.at[which * PIECES + k],
            device_id=above_device, device_id_type=MESH,
        )

    def owner_copy(k, i):
        c = lax.rem(k, WIDE // PART) * (PART // 8) + i
        q = lax.div(k, WIDE // PART)
        return c, q, pltpu.make_async_remote_copy(
            src_ref=upper_sum.at[at(k * PART + i * 8, 8, 8), :],
            dst_ref=in_root.at[at(q * 8, 8, 8), at(offset, COLS, COLS)],
            send_sem=root_send.at[k * (PART // 8) + i], recv_sem=root_recv.at[q * 4 + lax.rem(me, 4)],
            device_id=(row, lax.div(c, 8), lax.rem(c, 8)), device_id_type=MESH,
        )

    def to_owners(k):
        def one(i, carry):
            c, q, out_copy = owner_copy(k, i)

            @pl.when(c != me)
            def _():
                out_copy.start()

            @pl.when(c == me)
            def _():
                in_root[at(q * 8, 8, 8), at(offset, COLS, COLS)] = upper_sum[at(k * PART + i * 8, 8, 8), :]

            return carry

        lax.fori_loop(0, PART // 8, one, 0)

    def sum_round(step):
        first = (step - SKEW * (DEPTH - depth)) * PACK

        @pl.when(member & (first >= 0) & (first < PIECES))
        def _():
            def one(i, carry):
                k = first + i
                for which, there in enumerate((child_up, child_down)):
                    @pl.when(there)
                    def _():
                        sum_copy(k, which).wait_recv()
                        mine = at(k * PART, PART, PART)
                        other = at(which * PIECES * PART + k * PART, PART, PART)
                        upper_sum[mine, :] = upper_sum[mine, :] + upper_in[other, :]

                @pl.when(below)
                def _():
                    sum_copy(k, slot).start()

                @pl.when(root)
                def _():
                    to_owners(k)

                return carry

            lax.fori_loop(0, PACK, one, 0)

    def prepare():
        def one(n, carry):
            rows = at(n * 256, 256, 256)
            pltpu.make_async_copy(upstream.at[rows, :], tile.at[rows, :], local_sem.at[n]).wait()
            row_number = row * ROWS + n * 256 + lax.broadcasted_iota(jnp.int32, (256, COLS), 0)
            col_number = me * COLS + lax.broadcasted_iota(jnp.int32, (256, COLS), 1)
            kept = jnp.where(col_number <= row_number, tile[rows, :], 0.0)
            tile_high[rows, :], tile_low[rows, :] = halves(kept)
            return carry

        lax.fori_loop(0, 8, one, 0)

        @pl.when(relay)
        def _():
            def clear_relay(n, carry):
                upper_sum[at(n * 64, 64, 64), :] = jnp.zeros((64, COLS), jnp.float32)
                return carry

            lax.fori_loop(0, 16, clear_relay, 0)

        @pl.when(jnp.logical_not(active))
        def _():
            def clear(n, carry):
                lower_sum[at(n * 64, 64, 64), :] = jnp.zeros((64, ROWS), jnp.float32)
                return carry

            lax.fori_loop(0, 16, clear, 0)

    def product(left_a, left_b, right_a, right_b, dims):
        dot = functools.partial(
            lax.dot_general, dimension_numbers=(dims, ((), ())), preferred_element_type=jnp.float32
        )
        return dot(left_a, right_a) + dot(left_b, right_a) + dot(left_a, right_b)

    def upper(q, n):
        @pl.when(active)
        def _():
            here = pl.ds(q * WIDE, WIDE)

            def cut(i, carry):
                cols = at(i * 256, 256, 256)
                left_high[:, cols], left_low[:, cols] = halves(gathered[here, cols])
                return carry

            if n == 0:
                lax.fori_loop(0, 8, cut, 0)
            cols = pl.ds(n * 256, 256)
            upper_sum[here, cols] = product(
                left_high[...], left_low[...], tile_high[:, cols], tile_low[:, cols], ((1,), (0,))
            )

    def lower(q, n):
        @pl.when(active)
        def _():
            here = pl.ds(q * WIDE, WIDE)
            if n == 0:
                @pl.when(root)
                def _():
                    right_high[...], right_low[...] = halves(gathered[here, at(offset, COLS, COLS)])

                @pl.when(below)
                def _():
                    right_high[...], right_low[...] = halves(block[here, :])

            def one(i, carry):
                rows = at(n * HALF + i * 256, 256, 256)
                lower_sum[here, rows] = product(
                    right_high[...], right_low[...], tile_high[rows, :], tile_low[rows, :], ((1,), (1,))
                )
                return carry

            lax.fori_loop(0, 4, one, 0)

    def scatter_partner(q, h):
        for half in range(2):
            send(
                group(lower_sum, q, half, 1 - core).at[:, columns(h)],
                in_partner.at[pl.ds((q * 2 + half) * 64, 64), columns(h)],
                2 * LANES + 2 * CHUNKS + (2 * q + h) * 2 + half, partner,
            )

    def scatter_far(q, h):
        base = LANES + (2 * q + h) * STAGES
        for half in range(2):
            came = pl.ds((q * 2 + half) * 64, 64)
            arrived(in_partner.at[came, columns(h)], 2 * LANES + 2 * CHUNKS + (2 * q + h) * 2 + half)
            mine = at(q * WIDE + half * 128 + core * 64, 64, 8)
            lower_sum[mine, columns(h)] = lower_sum[mine, columns(h)] + in_partner[came, columns(h)]
        for j in (3, 1, 2, 0):
            for way, step in enumerate((1, 3)):
                send(
                    total(q, chip(h, AWAY[j], 2), quarter(h, way)),
                    in_far.at[pl.ds((q * 8 + 2 * j + way) * 8, 8), pl.ds(h * (HALF // 2), HALF // 2)],
                    base + 2 * j + way, device(chip(h, 0, step), core),
                )

    def scatter_near(q, h):
        base = LANES + (2 * q + h) * STAGES
        for j in (3, 1, 2, 0):
            for way, step in enumerate((1, 3)):
                to = chip(h, AWAY[j], step)
                came = pl.ds((q * 8 + 2 * j + way) * 8, 8)
                came_cols = pl.ds(h * (HALF // 2), HALF // 2)
                arrived(in_far.at[came, came_cols], base + 2 * j + way)
                mine, cols = at(q * WIDE + number(to), 8, 8), quarter(h, way)
                lower_sum[mine, cols] = lower_sum[mine, cols] + in_far[came, came_cols]
                send(
                    total(q, to, columns(h)), in_near.at[came, columns(h)], base + 8 + 2 * j + way,
                    device(chip(h, 0, step), core),
                )

    def scatter_column(q, h):
        base, cols = LANES + (2 * q + h) * STAGES, columns(h)
        for j in (3, 1, 2, 0):
            mine = at(q * WIDE + number(chip(h, AWAY[j], 0)), 8, 8)
            first, second = (pl.ds((q * 8 + 2 * j + way) * 8, 8) for way in range(2))
            arrived(in_near.at[first, cols], base + 8 + 2 * j)
            arrived(in_near.at[second, cols], base + 8 + 2 * j + 1)
            lower_sum[mine, cols] = lower_sum[mine, cols] + (in_near[first, cols] + in_near[second, cols])
            if j == 3:
                for way, step in enumerate((1, 3)):
                    send(
                        total(q, chip(h, 2, 0), quarter(h, way)),
                        in_cross_far.at[pl.ds((q * 2 + way) * 8, 8), pl.ds(h * (HALF // 2), HALF // 2)],
                        base + 16 + way, device(chip(h, step, 0), core),
                    )

    def scatter_row(q, h):
        base = LANES + (2 * q + h) * STAGES
        for way, step in enumerate((1, 3)):
            to = chip(h, step, 0)
            came = pl.ds((q * 2 + way) * 8, 8)
            came_cols = pl.ds(h * (HALF // 2), HALF // 2)
            arrived(in_cross_far.at[came, came_cols], base + 16 + way)
            mine, cols = at(q * WIDE + number(to), 8, 8), quarter(h, way)
            lower_sum[mine, cols] = lower_sum[mine, cols] + in_cross_far[came, came_cols]
            send(total(q, to, columns(h)), in_cross.at[came, columns(h)], base + 18 + way, device(to, core))

    def scatter_done(q, h):
        base, cols = LANES + (2 * q + h) * STAGES, columns(h)
        first, second = (pl.ds((q * 2 + way) * 8, 8) for way in range(2))
        arrived(in_cross.at[first, cols], base + 18)
        arrived(in_cross.at[second, cols], base + 19)
        mine = at(q * WIDE + me * 8, 8, 8)
        out[pl.ds(q * 8, 8), cols] = lower_sum[mine, cols] + (in_cross[first, cols] + in_cross[second, cols])

    def finish(q):
        here = pl.ds(q * 8, 8)
        for g in range(4):
            cols = pl.ds(g * COLS, COLS)

            @pl.when(me != row * 4 + g)
            def _():
                piece = in_root.at[here, cols]
                pltpu.make_async_remote_copy(
                    src_ref=piece, dst_ref=piece, send_sem=root_send.at[0], recv_sem=root_recv.at[q * 4 + g],
                    device_id=partner, device_id_type=MESH,
                ).wait_recv()

        out[here, :] = out[here, :] + in_root[here, :]

    def fetch(n, carry):
        rows = at(n * 256, 256, 256)
        pltpu.make_async_copy(upstream.at[rows, :], tile.at[rows, :], local_sem.at[n]).start()
        return carry

    lax.fori_loop(0, 8, fetch, 0)
    for q in range(CHUNKS):
        gathered[at(q * WIDE + me * 8, 8, 8), :] = panel[pl.ds(q * 8, 8), :]

    barrier = pltpu.get_barrier_semaphore()

    def greet(to):
        pl.semaphore_signal(barrier, inc=1, device_id=to, device_id_type=MESH)

    for first, second in ((1, 0), (3, 0), (0, 1), (0, 3)):
        greet(device(chip(0, first, second), core))
    greet(partner)
    for there, to in ((below, above_device), (child_up, up_device), (child_down, down_device)):
        @pl.when(there)
        def _():
            greet(to)

    for g in range(4):
        @pl.when(me != row * 4 + g)
        def _():
            c = row * 4 + g
            greet((row, lax.div(c, 8), lax.rem(c, 8)))

    pl.semaphore_wait(
        barrier, 5 + jnp.where(root, 31, 0) + sum(jnp.where(there, 1, 0) for there in (below, child_up, child_down))
    )

    plan = []

    def add(time, tag, task, *args):
        if tag in ON:
            plan.append((time, len(plan), functools.partial(task, *args)))

    schedule(add, locals())
    for _, _, task in sorted(plan, key=lambda entry: entry[:2]):
        task()

    for one in sent:
        one.wait_send()

    def settle(k, carry):
        if "z" in ON:
            @pl.when(child_up)
            def _():
                z_copy(part(block, k), k, 0, up_device).wait_send()

            @pl.when(child_down)
            def _():
                z_copy(part(block, k), k, 1, down_device).wait_send()

        if "r" in ON:
            @pl.when(below)
            def _():
                sum_copy(k, 0).wait_send()

            @pl.when(root)
            def _():
                for i in range(PART // 8):
                    c, _, out_copy = owner_copy(k, i)

                    @pl.when(c != me)
                    def _():
                        out_copy.wait_send()

        return carry

    lax.fori_loop(0, PIECES, settle, 0)


ON = "gpzruls"
GAP, LAST = 5.4, 0.0
GATHER = (0.0, 4.5, 6.0, 7.5, 9.0, 10.0, 12.0, 15.0, 17.5)
Z0, DZ, R0, DR = 21.0, 1.4, 30.0, 1.6
LOW0, LOWGAP = 43.0, 5.6
SCATTER = (1.3, 4.0, 7.0, 10.5, 13.5, 17.0)
FINISH = 200.0


def schedule(add, do):
    for q in range(CHUNKS):
        tasks = [
            (do["gather_own"], q), (do["gather_first"], q), (do["gather_forward"], q, 0), (do["gather_opposite"], q),
            (do["gather_forward"], q, 1), (do["gather_forward"], q, 2), (do["gather_forward"], q, 3),
            (do["gather_last"], q), (do["gather_done"], q),
        ]
        for time, task in zip(GATHER, tasks):
            add(GAP * q + time, "g", *task)
        done = GAP * q + GATHER[-1]
        add(done, "z", do["z_start"], q)
        for n in range(2):
            add(done + 0.1 + 1.3 * n, "u", do["upper"], q, n)
            low = LOW0 + LOWGAP * q + 1.8 * n
            add(low, "l", do["lower"], q, n)
            for time, stage in zip(SCATTER, ("partner", "far", "near", "column", "row", "done")):
                add(low + time, "s", do["scatter_" + stage], q, n)
        add(FINISH + q, "r", do["finish"], q)
    add(0.5, "p", do["prepare"])
    for n in range(PIECES // PACK + SKEW * (DEPTH - 1)):
        add(Z0 + DZ * n, "z", do["z_round"], n)
    for n in range(PIECES // PACK + SKEW * DEPTH):
        add(R0 + DR * n, "r", do["sum_round"], n)


def per_device(upstream, input_panel):
    f32, bf16 = jnp.float32, jnp.bfloat16
    total = CHUNKS * WIDE
    vmem = pltpu.VMEM
    result = pl.pallas_call(
        kernel,
        out_shape=jax.ShapeDtypeStruct((32, ROWS), f32),
        in_specs=[pl.BlockSpec(memory_space=pl.ANY), pl.BlockSpec(memory_space=pltpu.VMEM)],
        out_specs=pl.BlockSpec(memory_space=pltpu.VMEM),
        scratch_shapes=[
            vmem((total, ROWS), f32),
            vmem((total, COLS), f32),
            vmem((total, COLS), f32),
            vmem((2 * total, COLS), f32),
            vmem((total, ROWS), f32),
            vmem((total // 2, ROWS), f32),
            vmem((CHUNKS * 64, HALF), f32),
            vmem((CHUNKS * 64, ROWS), f32),
            vmem((CHUNKS * 16, HALF), f32),
            vmem((CHUNKS * 16, ROWS), f32),
            vmem((CHUNKS * 8, ROWS), f32),
            vmem((ROWS, COLS), f32),
            vmem((ROWS, COLS), bf16),
            vmem((ROWS, COLS), bf16),
            vmem((WIDE, ROWS), bf16),
            vmem((WIDE, ROWS), bf16),
            vmem((WIDE, COLS), bf16),
            vmem((WIDE, COLS), bf16),
            pltpu.SemaphoreType.DMA((COPIES,)),
            pltpu.SemaphoreType.DMA((COPIES,)),
            pltpu.SemaphoreType.DMA((3 * PIECES,)),
            pltpu.SemaphoreType.DMA((PIECES,)),
            pltpu.SemaphoreType.DMA((2 * PIECES,)),
            pltpu.SemaphoreType.DMA((PIECES * PART // 8,)),
            pltpu.SemaphoreType.DMA((CHUNKS * 4,)),
            pltpu.SemaphoreType.DMA((8,)),
        ],
        compiler_params=pltpu.CompilerParams(
            collective_id=0, has_side_effects=True, vmem_limit_bytes=60 * 1024 * 1024
        ),
    )(upstream, input_panel.T)
    return result.T


def solution(mesh):
    placed = (P("row", ("col", "rep")), P("row", ("col", "rep")))
    return jax.shard_map(
        per_device, mesh=mesh, in_specs=placed, out_specs=P("row", ("col", "rep")), check_vma=False
    )
```

time: 144 us -> 124 us (0.86)
  the two profiles are of different devices: /device:TPU:1 before, /device:TPU:41 now
where the time goes in v2:
time: 124 us; the launch traced here: 123 us
  Pallas kernels  122 us (98%)
  local copies, waits for them, and re-layouts  1.67 us (1%)
    pallas_call x1, Pallas kernels, per_device(): pl.pallas_call(kernel, out_shape=jax.ShapeDtypeStruct((32, ROWS), f32), i...  122 us

profile of v2, /device:TPU:41, one launch (start us, length us, event | category | flops | bytes accessed | tf_op | source)
XLA Modules:
  0.0 123.4 jit_solution(17167085937521039044)
XLA Ops:
  0.0 121.8 %shard_map.28 = f32[32,2048]{1,0:T(8,128)} custom-call(f32[2048,512]{1,0:T(8,128)} %upstream.1, f32[32,2048]{1,0:T(8,128)} %bitcast.3), custom_call_target="tpu_custom_call" | custom-call | tf_op jit(solution)/shard_map/pallas_call | solution.py:557
  121.8 1.7 %copy.4 = f32[2048,32]{0,1:T(8,128)} copy(f32[2048,32]{0,1:T(8,128)} %bitcast.2) | data formatting | bytes 524288

commit v3 on v2

--- a/solution.py
+++ b/solution.py
@@ -15,7 +15,7 @@
 WIDE = 256
 PIECES = 32
 PART = 32
-PACK = 2
+PACK = 1
 DEPTH = 5
 SKEW = 3
 AWAY = (0, 3, 1, 2)
@@ -474,21 +474,15 @@
         barrier, 5 + jnp.where(root, 31, 0) + sum(jnp.where(there, 1, 0) for there in (below, child_up, child_down))
     )
 
-    plan = []
-
-    def add(time, tag, task, *args):
-        if tag in ON:
-            plan.append((time, len(plan), functools.partial(task, *args)))
-
-    schedule(add, locals())
-    for _, _, task in sorted(plan, key=lambda entry: entry[:2]):
-        task()
+    tasks = locals()
+    for which, *args in ORDER:
+        tasks[TASKS[which]](*args)
 
     for one in sent:
         one.wait_send()
 
     def settle(k, carry):
-        if "z" in ON:
+        if True:
             @pl.when(child_up)
             def _():
                 z_copy(part(block, k), k, 0, up_device).wait_send()
@@ -497,7 +491,7 @@
             def _():
                 z_copy(part(block, k), k, 1, down_device).wait_send()
 
-        if "r" in ON:
+        if True:
             @pl.when(below)
             def _():
                 sum_copy(k, 0).wait_send()
@@ -516,38 +510,49 @@
     lax.fori_loop(0, PIECES, settle, 0)
 
 
-ON = "gpzruls"
-GAP, LAST = 5.4, 0.0
-GATHER = (0.0, 4.5, 6.0, 7.5, 9.0, 10.0, 12.0, 15.0, 17.5)
-Z0, DZ, R0, DR = 21.0, 1.4, 30.0, 1.6
-LOW0, LOWGAP = 43.0, 5.6
-SCATTER = (1.3, 4.0, 7.0, 10.5, 13.5, 17.0)
-FINISH = 200.0
-
-
-def schedule(add, do):
-    for q in range(CHUNKS):
-        tasks = [
-            (do["gather_own"], q), (do["gather_first"], q), (do["gather_forward"], q, 0), (do["gather_opposite"], q),
-            (do["gather_forward"], q, 1), (do["gather_forward"], q, 2), (do["gather_forward"], q, 3),
-            (do["gather_last"], q), (do["gather_done"], q),
-        ]
-        for time, task in zip(GATHER, tasks):
-            add(GAP * q + time, "g", *task)
-        done = GAP * q + GATHER[-1]
-        add(done, "z", do["z_start"], q)
-        for n in range(2):
-            add(done + 0.1 + 1.3 * n, "u", do["upper"], q, n)
-            low = LOW0 + LOWGAP * q + 1.8 * n
-            add(low, "l", do["lower"], q, n)
-            for time, stage in zip(SCATTER, ("partner", "far", "near", "column", "row", "done")):
-                add(low + time, "s", do["scatter_" + stage], q, n)
-        add(FINISH + q, "r", do["finish"], q)
-    add(0.5, "p", do["prepare"])
-    for n in range(PIECES // PACK + SKEW * (DEPTH - 1)):
-        add(Z0 + DZ * n, "z", do["z_round"], n)
-    for n in range(PIECES // PACK + SKEW * DEPTH):
-        add(R0 + DR * n, "r", do["sum_round"], n)
+TASKS = (
+    "gather_own",
+    "prepare",
+    "gather_first",
+    "gather_opposite",
+    "gather_forward",
+    "gather_last",
+    "gather_done",
+    "z_start",
+    "upper",
+    "z_round",
+    "sum_round",
+    "lower",
+    "scatter_partner",
+    "scatter_far",
+    "scatter_near",
+    "scatter_column",
+    "scatter_row",
+    "scatter_done",
+    "finish",
+)
+ORDER = (
+    (0, 0), (1,), (2, 0), (0, 1), (3, 0), (4, 0, 0), (4, 0, 1), (2, 1), (4, 0, 2), (4, 0, 3), (4, 1, 0),
+    (3, 1), (0, 2), (4, 1, 2), (5, 0), (2, 2), (6, 0), (7, 0), (4, 1, 3), (4, 1, 1), (0, 3), (8, 0, 0),
+    (9, 0), (8, 0, 1), (9, 1), (3, 2), (4, 2, 0), (5, 1), (9, 2), (2, 3), (4, 2, 2), (9, 3), (9, 4), (9, 5),
+    (10, 0), (6, 1), (4, 2, 3), (7, 1), (10, 1), (10, 2), (4, 2, 1), (9, 6), (8, 1, 0), (10, 3), (10, 4),
+    (9, 7), (9, 8), (5, 2), (4, 3, 0), (3, 3), (10, 5), (9, 9), (8, 1, 1), (10, 6), (9, 10), (10, 7), (6, 2),
+    (9, 11), (4, 3, 1), (7, 2), (10, 8), (8, 2, 0), (10, 9), (9, 12), (9, 13), (10, 10), (4, 3, 2), (4, 3, 3),
+    (9, 14), (8, 2, 1), (9, 15), (10, 11), (9, 16), (5, 3), (9, 17), (10, 12), (9, 18), (10, 13), (9, 19),
+    (6, 3), (9, 20), (10, 14), (8, 3, 0), (9, 21), (7, 3), (10, 15), (9, 22), (11, 0, 0), (12, 0, 0),
+    (10, 16), (9, 23), (11, 0, 1), (12, 0, 1), (9, 24), (9, 25), (10, 17), (9, 26), (10, 18), (13, 0, 0),
+    (8, 3, 1), (9, 27), (10, 19), (13, 0, 1), (9, 28), (11, 1, 0), (9, 29), (10, 20), (10, 21), (12, 1, 0),
+    (9, 30), (11, 1, 1), (9, 31), (10, 22), (14, 0, 0), (12, 1, 1), (10, 23), (9, 32), (10, 24), (14, 0, 1),
+    (13, 1, 0), (9, 33), (10, 25), (13, 1, 1), (15, 0, 0), (9, 34), (10, 26), (9, 35), (11, 2, 0), (10, 27),
+    (10, 28), (9, 36), (9, 37), (15, 0, 1), (14, 1, 0), (10, 29), (12, 2, 0), (14, 1, 1), (11, 2, 1), (9, 38),
+    (12, 2, 1), (10, 30), (9, 39), (10, 31), (13, 2, 1), (13, 2, 0), (9, 40), (10, 32), (16, 0, 1), (9, 41),
+    (15, 1, 0), (10, 33), (16, 0, 0), (15, 1, 1), (9, 42), (10, 34), (9, 43), (11, 3, 0), (10, 35),
+    (14, 2, 0), (12, 3, 0), (14, 2, 1), (11, 3, 1), (17, 0, 0), (12, 3, 1), (10, 36), (10, 37), (10, 38),
+    (13, 3, 0), (13, 3, 1), (16, 1, 0), (10, 39), (15, 2, 1), (10, 40), (15, 2, 0), (10, 41), (14, 3, 0),
+    (14, 3, 1), (10, 42), (16, 2, 1), (16, 1, 1), (10, 43), (16, 2, 0), (15, 3, 0), (15, 3, 1), (10, 44),
+    (10, 45), (17, 0, 1), (10, 46), (18, 0), (16, 3, 0), (17, 2, 0), (17, 1, 0), (16, 3, 1), (17, 3, 0),
+    (17, 2, 1), (17, 1, 1), (18, 2), (18, 1), (17, 3, 1), (18, 3),
+)
 
 
 def per_device(upstream, input_panel):

time: 124 us -> 117 us (0.944)
  the two profiles are of different devices: /device:TPU:41 before, /device:TPU:1 now
where the time goes in v3:
time: 117 us; the launch traced here: 116 us
  Pallas kernels  114 us (97%)
  local copies, waits for them, and re-layouts  1.67 us (1%)
    pallas_call x1, Pallas kernels, per_device(): pl.pallas_call(kernel, out_shape=jax.ShapeDtypeStruct((32, ROWS), f32), i...  114 us

profile of v3, /device:TPU:1, one launch (start us, length us, event | category | flops | bytes accessed | tf_op | source)
XLA Modules:
  0.0 115.6 jit_solution(2449714709283706869)
XLA Ops:
  0.0 114.0 %shard_map.28 = f32[32,2048]{1,0:T(8,128)} custom-call(f32[2048,512]{1,0:T(8,128)} %upstream.1, f32[32,2048]{1,0:T(8,128)} %bitcast.3), custom_call_target="tpu_custom_call" | custom-call | tf_op jit(solution)/shard_map/pallas_call | solution.py:562
  114.0 1.7 %copy.4 = f32[2048,32]{0,1:T(8,128)} copy(f32[2048,32]{0,1:T(8,128)} %bitcast.2) | data formatting | bytes 524288

commit v4 on v3

--- a/solution.py
+++ b/solution.py
@@ -35,10 +35,10 @@
 
 def kernel(
     upstream, panel, out,
-    gathered, block, upper_sum, upper_in, lower_sum,
+    gathered, block, upper_sum, side_sum, upper_in, lower_sum,
     in_partner, in_far, in_near, in_cross_far, in_cross, in_root,
     tile, tile_high, tile_low, left_high, left_low, right_high, right_low,
-    send_sem, recv_sem, z_send, z_down, z_up, root_send, root_recv, local_sem,
+    send_sem, recv_sem, z_send, z_down, z_up, root_send, root_recv, side_send, side_recv, local_sem,
 ):
     row, col, rep = lax.axis_index("row"), lax.axis_index("col"), lax.axis_index("rep")
     core, x = lax.rem(col, 2), lax.div(rep, 2)
@@ -62,22 +62,28 @@
 
     low = lax.div(col, 2) * 4 + lax.div(x, 2)
     high = low + 2
-    source = jnp.where(core == 0, low, high)
     offset = lax.rem(me, 4) * COLS
-    active = row >= source
-    root = row == source
-    relay = (core == 0) & (low == 4) & (row == 2)
-    below = (row > source) | relay
-    member = active | relay
-    upward = (core == 1) | (row <= high)
-    child_up = ((core == 0) & (row >= low) & (row < high)) | ((core == 1) & (row >= high) & (row < 7))
-    child_down = ((core == 0) & ((root & (high < 7)) | (row > high + 1))) | relay
-    depth = jnp.where(relay, 1, jnp.where(upward, row - source, 8 - row + jnp.where(low == 4, 1, 0)))
-    above = jnp.where(relay, 4, jnp.where(upward, row - 1, jnp.where(row < 7, row + 1, jnp.where(low == 4, 2, low))))
+
+    def line(first):
+        second = jnp.logical_not(first)
+        source = jnp.where(first, low, high)
+        relay = first & (low == 4) & (row == 2)
+        root, active = row == source, row >= source
+        upward = second | (row <= high)
+        child_up = (first & (row >= low) & (row < high)) | (second & (row >= high) & (row < 7))
+        child_down = (first & ((root & (high < 7)) | (row > high + 1))) | relay
+        depth = jnp.where(relay, 1, jnp.where(upward, row - source, 8 - row + jnp.where(low == 4, 1, 0)))
+        far = jnp.where(row < 7, row + 1, jnp.where(low == 4, 2, low))
+        above = jnp.where(relay, 4, jnp.where(upward, row - 1, far))
+        down = jnp.where(root & (low == 4), 2, jnp.where(root | relay, 7, row - 1))
+        slot = jnp.where(upward & jnp.logical_not(relay), 0, 1)
+        return root, active, relay, active & jnp.logical_not(root) | relay, child_up, child_down, depth, above, down, slot
+
+    root, active, _, below, child_up, child_down, depth, above, down, _ = line(core == 0)
+    sum_root, sum_active, sum_relay, sum_below, sum_up, sum_down, sum_depth, sum_above, sum_below_row, sum_slot = line(core == 1)
     up_device = (row + 1, col, rep)
-    down_device = (jnp.where(root & (low == 4), 2, jnp.where(root | relay, 7, row - 1)), col, rep)
+    down_device = (down, col, rep)
     above_device = (above, col, rep)
-    slot = jnp.where(upward & jnp.logical_not(relay), 0, 1)
 
     def copy(src, dst, which, to):
         return pltpu.make_async_remote_copy(
@@ -223,16 +229,16 @@
 
     def sum_copy(k, which):
         return pltpu.make_async_remote_copy(
-            src_ref=part(upper_sum, k), dst_ref=part(upper_in, k, which * PIECES * PART),
+            src_ref=part(side_sum, k), dst_ref=part(upper_in, k, which * PIECES * PART),
             send_sem=z_send.at[2 * PIECES + k], recv_sem=z_up.at[which * PIECES + k],
-            device_id=above_device, device_id_type=MESH,
+            device_id=(sum_above, col, rep), device_id_type=MESH,
         )
 
     def owner_copy(k, i):
         c = lax.rem(k, WIDE // PART) * (PART // 8) + i
         q = lax.div(k, WIDE // PART)
         return c, q, pltpu.make_async_remote_copy(
-            src_ref=upper_sum.at[at(k * PART + i * 8, 8, 8), :],
+            src_ref=side_sum.at[at(k * PART + i * 8, 8, 8), :],
             dst_ref=in_root.at[at(q * 8, 8, 8), at(offset, COLS, COLS)],
             send_sem=root_send.at[k * (PART // 8) + i], recv_sem=root_recv.at[q * 4 + lax.rem(me, 4)],
             device_id=(row, lax.div(c, 8), lax.rem(c, 8)), device_id_type=MESH,
@@ -248,32 +254,49 @@
 
             @pl.when(c == me)
             def _():
-                in_root[at(q * 8, 8, 8), at(offset, COLS, COLS)] = upper_sum[at(k * PART + i * 8, 8, 8), :]
+                in_root[at(q * 8, 8, 8), at(offset, COLS, COLS)] = side_sum[at(k * PART + i * 8, 8, 8), :]
 
             return carry
 
         lax.fori_loop(0, PART // 8, one, 0)
 
+    def side_copy(q):
+        rows = pl.ds(q * WIDE, WIDE)
+        return pltpu.make_async_remote_copy(
+            src_ref=upper_sum.at[rows, :], dst_ref=side_sum.at[rows, :], send_sem=side_send.at[q],
+            recv_sem=side_recv.at[q], device_id=partner, device_id_type=MESH,
+        )
+
+    def hand_over(q):
+        @pl.when(active)
+        def _():
+            side_copy(q).start()
+
+    def take_over(q):
+        @pl.when(sum_active)
+        def _():
+            side_copy(q).wait_recv()
+
     def sum_round(step):
-        first = (step - SKEW * (DEPTH - depth)) * PACK
-
-        @pl.when(member & (first >= 0) & (first < PIECES))
+        first = (step - SKEW * (DEPTH - sum_depth)) * PACK
+
+        @pl.when((sum_active | sum_relay) & (first >= 0) & (first < PIECES))
         def _():
             def one(i, carry):
                 k = first + i
-                for which, there in enumerate((child_up, child_down)):
+                for which, there in enumerate((sum_up, sum_down)):
                     @pl.when(there)
                     def _():
                         sum_copy(k, which).wait_recv()
                         mine = at(k * PART, PART, PART)
                         other = at(which * PIECES * PART + k * PART, PART, PART)
-                        upper_sum[mine, :] = upper_sum[mine, :] + upper_in[other, :]
-
-                @pl.when(below)
-                def _():
-                    sum_copy(k, slot).start()
-
-                @pl.when(root)
+                        side_sum[mine, :] = side_sum[mine, :] + upper_in[other, :]
+
+                @pl.when(sum_below)
+                def _():
+                    sum_copy(k, sum_slot).start()
+
+                @pl.when(sum_root)
                 def _():
                     to_owners(k)
 
@@ -293,10 +316,10 @@
 
         lax.fori_loop(0, 8, one, 0)
 
-        @pl.when(relay)
+        @pl.when(sum_relay)
         def _():
             def clear_relay(n, carry):
-                upper_sum[at(n * 64, 64, 64), :] = jnp.zeros((64, COLS), jnp.float32)
+                side_sum[at(n * 64, 64, 64), :] = jnp.zeros((64, COLS), jnp.float32)
                 return carry
 
             lax.fori_loop(0, 16, clear_relay, 0)
@@ -427,12 +450,16 @@
         mine = at(q * WIDE + me * 8, 8, 8)
         out[pl.ds(q * 8, 8), cols] = lower_sum[mine, cols] + (in_cross[first, cols] + in_cross[second, cols])
 
+    def summer(g):
+        c = row * 4 + g
+        return c + 8 - 16 * lax.rem(lax.div(c, 8), 2)
+
     def finish(q):
         here = pl.ds(q * 8, 8)
         for g in range(4):
             cols = pl.ds(g * COLS, COLS)
 
-            @pl.when(me != row * 4 + g)
+            @pl.when(me != summer(g))
             def _():
                 piece = in_root.at[here, cols]
                 pltpu.make_async_remote_copy(
@@ -459,19 +486,21 @@
     for first, second in ((1, 0), (3, 0), (0, 1), (0, 3)):
         greet(device(chip(0, first, second), core))
     greet(partner)
-    for there, to in ((below, above_device), (child_up, up_device), (child_down, down_device)):
+    met = (below, child_up, child_down, sum_below, sum_up, sum_down)
+    rows_met = (above, row + 1, down, sum_above, row + 1, sum_below_row)
+    for there, to_row in zip(met, rows_met):
         @pl.when(there)
         def _():
-            greet(to)
+            greet((to_row, col, rep))
 
     for g in range(4):
-        @pl.when(me != row * 4 + g)
-        def _():
-            c = row * 4 + g
+        @pl.when(me != summer(g))
+        def _():
+            c = summer(g)
             greet((row, lax.div(c, 8), lax.rem(c, 8)))
 
     pl.semaphore_wait(
-        barrier, 5 + jnp.where(root, 31, 0) + sum(jnp.where(there, 1, 0) for there in (below, child_up, child_down))
+        barrier, 5 + jnp.where(sum_root, 31, 0) + sum(jnp.where(there, 1, 0) for there in met)
     )
 
     tasks = locals()
@@ -492,11 +521,11 @@
                 z_copy(part(block, k), k, 1, down_device).wait_send()
 
         if True:
-            @pl.when(below)
+            @pl.when(sum_below)
             def _():
                 sum_copy(k, 0).wait_send()
 
-            @pl.when(root)
+            @pl.when(sum_root)
             def _():
                 for i in range(PART // 8):
                     c, _, out_copy = owner_copy(k, i)
@@ -508,6 +537,10 @@
         return carry
 
     lax.fori_loop(0, PIECES, settle, 0)
+    for q in range(CHUNKS):
+        @pl.when(active)
+        def _():
+            side_copy(q).wait_send()
 
 
 TASKS = (
@@ -521,6 +554,8 @@
     "z_start",
     "upper",
     "z_round",
+    "hand_over",
+    "take_over",
     "sum_round",
     "lower",
     "scatter_partner",
@@ -532,26 +567,27 @@
     "finish",
 )
 ORDER = (
-    (0, 0), (1,), (2, 0), (0, 1), (3, 0), (4, 0, 0), (4, 0, 1), (2, 1), (4, 0, 2), (4, 0, 3), (4, 1, 0),
-    (3, 1), (0, 2), (4, 1, 2), (5, 0), (2, 2), (6, 0), (7, 0), (4, 1, 3), (4, 1, 1), (0, 3), (8, 0, 0),
-    (9, 0), (8, 0, 1), (9, 1), (3, 2), (4, 2, 0), (5, 1), (9, 2), (2, 3), (4, 2, 2), (9, 3), (9, 4), (9, 5),
-    (10, 0), (6, 1), (4, 2, 3), (7, 1), (10, 1), (10, 2), (4, 2, 1), (9, 6), (8, 1, 0), (10, 3), (10, 4),
-    (9, 7), (9, 8), (5, 2), (4, 3, 0), (3, 3), (10, 5), (9, 9), (8, 1, 1), (10, 6), (9, 10), (10, 7), (6, 2),
-    (9, 11), (4, 3, 1), (7, 2), (10, 8), (8, 2, 0), (10, 9), (9, 12), (9, 13), (10, 10), (4, 3, 2), (4, 3, 3),
-    (9, 14), (8, 2, 1), (9, 15), (10, 11), (9, 16), (5, 3), (9, 17), (10, 12), (9, 18), (10, 13), (9, 19),
-    (6, 3), (9, 20), (10, 14), (8, 3, 0), (9, 21), (7, 3), (10, 15), (9, 22), (11, 0, 0), (12, 0, 0),
-    (10, 16), (9, 23), (11, 0, 1), (12, 0, 1), (9, 24), (9, 25), (10, 17), (9, 26), (10, 18), (13, 0, 0),
-    (8, 3, 1), (9, 27), (10, 19), (13, 0, 1), (9, 28), (11, 1, 0), (9, 29), (10, 20), (10, 21), (12, 1, 0),
-    (9, 30), (11, 1, 1), (9, 31), (10, 22), (14, 0, 0), (12, 1, 1), (10, 23), (9, 32), (10, 24), (14, 0, 1),
-    (13, 1, 0), (9, 33), (10, 25), (13, 1, 1), (15, 0, 0), (9, 34), (10, 26), (9, 35), (11, 2, 0), (10, 27),
-    (10, 28), (9, 36), (9, 37), (15, 0, 1), (14, 1, 0), (10, 29), (12, 2, 0), (14, 1, 1), (11, 2, 1), (9, 38),
-    (12, 2, 1), (10, 30), (9, 39), (10, 31), (13, 2, 1), (13, 2, 0), (9, 40), (10, 32), (16, 0, 1), (9, 41),
-    (15, 1, 0), (10, 33), (16, 0, 0), (15, 1, 1), (9, 42), (10, 34), (9, 43), (11, 3, 0), (10, 35),
-    (14, 2, 0), (12, 3, 0), (14, 2, 1), (11, 3, 1), (17, 0, 0), (12, 3, 1), (10, 36), (10, 37), (10, 38),
-    (13, 3, 0), (13, 3, 1), (16, 1, 0), (10, 39), (15, 2, 1), (10, 40), (15, 2, 0), (10, 41), (14, 3, 0),
-    (14, 3, 1), (10, 42), (16, 2, 1), (16, 1, 1), (10, 43), (16, 2, 0), (15, 3, 0), (15, 3, 1), (10, 44),
-    (10, 45), (17, 0, 1), (10, 46), (18, 0), (16, 3, 0), (17, 2, 0), (17, 1, 0), (16, 3, 1), (17, 3, 0),
-    (17, 2, 1), (17, 1, 1), (18, 2), (18, 1), (17, 3, 1), (18, 3),
+    (0, 0), (1,), (2, 0), (0, 1), (3, 0), (4, 0, 0), (4, 0, 1), (4, 0, 2), (2, 1), (4, 0, 3), (4, 1, 0),
+    (0, 2), (3, 1), (5, 0), (2, 2), (4, 1, 2), (4, 1, 1), (4, 1, 3), (6, 0), (7, 0), (8, 0, 0), (0, 3),
+    (3, 2), (8, 0, 1), (4, 2, 0), (9, 0), (9, 1), (10, 0), (4, 2, 1), (5, 1), (11, 0), (9, 2), (2, 3),
+    (12, 0), (9, 3), (4, 2, 3), (12, 1), (4, 2, 2), (6, 1), (9, 4), (8, 1, 0), (12, 2), (9, 5), (9, 6),
+    (7, 1), (8, 1, 1), (12, 3), (12, 4), (3, 3), (4, 3, 0), (4, 3, 2), (9, 7), (4, 3, 1), (10, 1), (9, 8),
+    (12, 5), (5, 2), (9, 9), (12, 6), (9, 10), (12, 7), (9, 11), (6, 2), (11, 1), (12, 8), (9, 12), (4, 3, 3),
+    (8, 2, 0), (9, 13), (12, 9), (12, 10), (7, 2), (8, 2, 1), (9, 14), (12, 11), (5, 3), (9, 15), (9, 16),
+    (12, 12), (10, 2), (6, 3), (12, 13), (9, 17), (7, 3), (8, 3, 0), (9, 18), (12, 14), (9, 19), (11, 2),
+    (12, 15), (13, 0, 0), (12, 16), (14, 0, 0), (9, 20), (9, 21), (8, 3, 1), (12, 17), (9, 22), (12, 18),
+    (13, 0, 1), (14, 0, 1), (9, 23), (12, 19), (15, 0, 0), (9, 24), (10, 3), (9, 25), (12, 20), (15, 0, 1),
+    (9, 26), (12, 21), (16, 0, 0), (12, 22), (9, 27), (13, 1, 0), (9, 28), (14, 1, 0), (12, 23), (11, 3),
+    (9, 29), (16, 0, 1), (12, 24), (13, 1, 1), (9, 30), (15, 1, 0), (14, 1, 1), (9, 31), (12, 25), (17, 0, 0),
+    (9, 32), (12, 26), (9, 33), (12, 27), (15, 1, 1), (9, 34), (16, 1, 0), (12, 28), (17, 0, 1), (9, 35),
+    (13, 2, 0), (9, 36), (18, 0, 0), (12, 29), (14, 2, 0), (12, 30), (16, 1, 1), (9, 37), (13, 2, 1),
+    (14, 2, 1), (9, 38), (15, 2, 0), (9, 39), (12, 31), (12, 32), (17, 1, 0), (18, 0, 1), (9, 40), (12, 33),
+    (15, 2, 1), (17, 1, 1), (9, 41), (12, 34), (9, 42), (16, 2, 0), (9, 43), (12, 35), (13, 3, 0), (14, 3, 0),
+    (12, 36), (18, 1, 0), (16, 2, 1), (13, 3, 1), (12, 37), (14, 3, 1), (12, 38), (15, 3, 0), (15, 3, 1),
+    (18, 1, 1), (19, 1, 0), (17, 2, 0), (12, 39), (19, 0, 1), (19, 0, 0), (12, 40), (17, 2, 1), (12, 41),
+    (16, 3, 0), (16, 3, 1), (12, 42), (12, 43), (18, 2, 1), (12, 44), (17, 3, 0), (17, 3, 1), (18, 2, 0),
+    (12, 45), (12, 46), (18, 3, 0), (18, 3, 1), (19, 2, 0), (19, 2, 1), (19, 1, 1), (20, 1), (20, 0),
+    (19, 3, 0), (20, 2), (19, 3, 1), (20, 3),
 )
 
 
@@ -566,6 +602,7 @@
         out_specs=pl.BlockSpec(memory_space=pltpu.VMEM),
         scratch_shapes=[
             vmem((total, ROWS), f32),
+            vmem((total, COLS), f32),
             vmem((total, COLS), f32),
             vmem((total, COLS), f32),
             vmem((2 * total, COLS), f32),
@@ -590,6 +627,8 @@
             pltpu.SemaphoreType.DMA((2 * PIECES,)),
             pltpu.SemaphoreType.DMA((PIECES * PART // 8,)),
             pltpu.SemaphoreType.DMA((CHUNKS * 4,)),
+            pltpu.SemaphoreType.DMA((CHUNKS,)),
+            pltpu.SemaphoreType.DMA((CHUNKS,)),
             pltpu.SemaphoreType.DMA((8,)),
         ],
         compiler_params=pltpu.CompilerParams(

time: 117 us -> 114 us (0.974)
  Pallas kernels: 114 us -> 110 us
    pallas_call x1, Pallas kernels: 114 us -> 110 us  [per_device(): pl.pallas_call(kernel, out_shape=jax.ShapeDtypeStruct((32, ROWS), f32), i...]
where the time goes in v4:
time: 114 us; the launch traced here: 112 us
  Pallas kernels  110 us (96%)
  local copies, waits for them, and re-layouts  1.67 us (1%)
    pallas_call x1, Pallas kernels, per_device(): pl.pallas_call(kernel, out_shape=jax.ShapeDtypeStruct((32, ROWS), f32), i...  110 us

profile of v4, /device:TPU:1, one launch (start us, length us, event | category | flops | bytes accessed | tf_op | source)
XLA Modules:
  0.0 112.1 jit_solution(18061588000281633696)
XLA Ops:
  0.0 110.4 %shard_map.28 = f32[32,2048]{1,0:T(8,128)} custom-call(f32[2048,512]{1,0:T(8,128)} %upstream.1, f32[32,2048]{1,0:T(8,128)} %bitcast.3), custom_call_target="tpu_custom_call" | custom-call | tf_op jit(solution)/shard_map/pallas_call | solution.py:598
  110.4 1.7 %copy.4 = f32[2048,32]{0,1:T(8,128)} copy(f32[2048,32]{0,1:T(8,128)} %bitcast.2) | data formatting | bytes 524288

commit v5 on v4

--- a/solution.py
+++ b/solution.py
@@ -19,6 +19,7 @@
 DEPTH = 5
 SKEW = 3
 AWAY = (0, 3, 1, 2)
+LAG = 40
 STAGES = 20
 LANES = 2 * CHUNKS * STAGES
 COPIES = 2 * LANES + 6 * CHUNKS
@@ -469,15 +470,6 @@
 
         out[here, :] = out[here, :] + in_root[here, :]
 
-    def fetch(n, carry):
-        rows = at(n * 256, 256, 256)
-        pltpu.make_async_copy(upstream.at[rows, :], tile.at[rows, :], local_sem.at[n]).start()
-        return carry
-
-    lax.fori_loop(0, 8, fetch, 0)
-    for q in range(CHUNKS):
-        gathered[at(q * WIDE + me * 8, 8, 8), :] = panel[pl.ds(q * 8, 8), :]
-
     barrier = pltpu.get_barrier_semaphore()
 
     def greet(to):
@@ -499,48 +491,67 @@
             c = summer(g)
             greet((row, lax.div(c, 8), lax.rem(c, 8)))
 
+    def fetch(n, carry):
+        rows = at(n * 256, 256, 256)
+        pltpu.make_async_copy(upstream.at[rows, :], tile.at[rows, :], local_sem.at[n]).start()
+        return carry
+
+    lax.fori_loop(0, 8, fetch, 0)
+    for q in range(CHUNKS):
+        gathered[at(q * WIDE + me * 8, 8, 8), :] = panel[pl.ds(q * 8, 8), :]
+
     pl.semaphore_wait(
         barrier, 5 + jnp.where(sum_root, 31, 0) + sum(jnp.where(there, 1, 0) for there in met)
     )
 
+    def settle_down(k, carry):
+        @pl.when(child_up)
+        def _():
+            z_copy(part(block, k), k, 0, up_device).wait_send()
+
+        @pl.when(child_down)
+        def _():
+            z_copy(part(block, k), k, 1, down_device).wait_send()
+
+        return carry
+
+    def settle_sum(k, carry):
+        @pl.when(sum_below)
+        def _():
+            sum_copy(k, 0).wait_send()
+
+        @pl.when(sum_root)
+        def _():
+            for i in range(PART // 8):
+                c, _, out_copy = owner_copy(k, i)
+
+                @pl.when(c != me)
+                def _():
+                    out_copy.wait_send()
+
+        return carry
+
+    early_pieces = PIECES - PIECES // CHUNKS
+    last_round = PIECES // PACK + SKEW * DEPTH - 1
     tasks = locals()
-    for which, *args in ORDER:
+    started, settled = [], 0
+    for n, (which, *args) in enumerate(ORDER):
         tasks[TASKS[which]](*args)
-
-    for one in sent:
+        started += [n] * (len(sent) - len(started))
+        while settled < len(sent) and started[settled] < n - LAG:
+            sent[settled].wait_send()
+            settled += 1
+        if TASKS[which] == "sum_round" and args[0] == last_round - 1:
+            lax.fori_loop(0, PIECES, settle_down, 0)
+            lax.fori_loop(0, early_pieces, settle_sum, 0)
+            for q in range(CHUNKS):
+                @pl.when(active)
+                def _():
+                    side_copy(q).wait_send()
+
+    for one in sent[settled:]:
         one.wait_send()
-
-    def settle(k, carry):
-        if True:
-            @pl.when(child_up)
-            def _():
-                z_copy(part(block, k), k, 0, up_device).wait_send()
-
-            @pl.when(child_down)
-            def _():
-                z_copy(part(block, k), k, 1, down_device).wait_send()
-
-        if True:
-            @pl.when(sum_below)
-            def _():
-                sum_copy(k, 0).wait_send()
-
-            @pl.when(sum_root)
-            def _():
-                for i in range(PART // 8):
-                    c, _, out_copy = owner_copy(k, i)
-
-                    @pl.when(c != me)
-                    def _():
-                        out_copy.wait_send()
-
-        return carry
-
-    lax.fori_loop(0, PIECES, settle, 0)
-    for q in range(CHUNKS):
-        @pl.when(active)
-        def _():
-            side_copy(q).wait_send()
+    lax.fori_loop(early_pieces, PIECES, settle_sum, 0)
 
 
 TASKS = (

time: 114 us -> 113 us (level)
  no operation moved by 1% of the time
where the time goes in v5:
time: 113 us; the launch traced here: 111 us
  Pallas kernels  110 us (97%)
  local copies, waits for them, and re-layouts  1.67 us (1%)
    pallas_call x1, Pallas kernels, per_device(): pl.pallas_call(kernel, out_shape=jax.ShapeDtypeStruct((32, ROWS), f32), i...  110 us

profile of v5, /device:TPU:1, one launch (start us, length us, event | category | flops | bytes accessed | tf_op | source)
XLA Modules:
  0.0 111.5 jit_solution(14967868587777495832)
XLA Ops:
  0.0 109.8 %shard_map.28 = f32[32,2048]{1,0:T(8,128)} custom-call(f32[2048,512]{1,0:T(8,128)} %upstream.1, f32[32,2048]{1,0:T(8,128)} %bitcast.3), custom_call_target="tpu_custom_call" | custom-call | tf_op jit(solution)/shard_map/pallas_call | solution.py:609
  109.8 1.7 %copy.4 = f32[2048,32]{0,1:T(8,128)} copy(f32[2048,32]{0,1:T(8,128)} %bitcast.2) | data formatting | bytes 524288

commit v6 on v5

--- a/solution.py
+++ b/solution.py
@@ -75,14 +75,14 @@
         child_down = (first & ((root & (high < 7)) | (row > high + 1))) | relay
         depth = jnp.where(relay, 1, jnp.where(upward, row - source, 8 - row + jnp.where(low == 4, 1, 0)))
         far = jnp.where(row < 7, row + 1, jnp.where(low == 4, 2, low))
-        above = jnp.where(relay, 4, jnp.where(upward, row - 1, far))
-        down = jnp.where(root & (low == 4), 2, jnp.where(root | relay, 7, row - 1))
+        above = jnp.where(relay, 4, jnp.where(upward, lax.rem(row + 7, 8), far))
+        down = jnp.where(root & (low == 4), 2, jnp.where(root | relay, 7, lax.rem(row + 7, 8)))
         slot = jnp.where(upward & jnp.logical_not(relay), 0, 1)
         return root, active, relay, active & jnp.logical_not(root) | relay, child_up, child_down, depth, above, down, slot
 
     root, active, _, below, child_up, child_down, depth, above, down, _ = line(core == 0)
     sum_root, sum_active, sum_relay, sum_below, sum_up, sum_down, sum_depth, sum_above, sum_below_row, sum_slot = line(core == 1)
-    up_device = (row + 1, col, rep)
+    up_device = (lax.rem(row + 1, 8), col, rep)
     down_device = (down, col, rep)
     above_device = (above, col, rep)
 
@@ -479,7 +479,7 @@
         greet(device(chip(0, first, second), core))
     greet(partner)
     met = (below, child_up, child_down, sum_below, sum_up, sum_down)
-    rows_met = (above, row + 1, down, sum_above, row + 1, sum_below_row)
+    rows_met = (above, up_device[0], down, sum_above, up_device[0], sum_below_row)
     for there, to_row in zip(met, rows_met):
         @pl.when(there)
         def _():

time: 113 us -> 113 us (level)
  no operation moved by 1% of the time
where the time goes in v6:
time: 113 us; the launch traced here: 111 us
  Pallas kernels  110 us (97%)
  local copies, waits for them, and re-layouts  1.67 us (1%)
    pallas_call x1, Pallas kernels, per_device(): pl.pallas_call(kernel, out_shape=jax.ShapeDtypeStruct((32, ROWS), f32), i...  110 us

profile of v6, /device:TPU:1, one launch (start us, length us, event | category | flops | bytes accessed | tf_op | source)
XLA Modules:
  0.0 111.5 jit_solution(2766623777758872267)
XLA Ops:
  0.0 109.8 %shard_map.28 = f32[32,2048]{1,0:T(8,128)} custom-call(f32[2048,512]{1,0:T(8,128)} %upstream.1, f32[32,2048]{1,0:T(8,128)} %bitcast.3), custom_call_target="tpu_custom_call" | custom-call | tf_op jit(solution)/shard_map/pallas_call | solution.py:609
  109.8 1.7 %copy.4 = f32[2048,32]{0,1:T(8,128)} copy(f32[2048,32]{0,1:T(8,128)} %bitcast.2) | data formatting | bytes 524288
